TPU v7x, 32 devices: a whole 2x2x4 slice. The times are simulated.
32 devices in a mesh: gx: 4 (over y, x), gy: 2 (over core), gz: 4 (over z).
Axes of the slice: x: 2, y: 2, z: 4, core: 2. Of those that a mesh axis runs over, the one named last changes fastest.
Arguments:
- gradient: bfloat16 [32, 32, 16, 512], P(None, 'gx', 'gy', 'gz'), may hold values from -6 to 6
- noise_draw: bfloat16 [32, 32, 16, 512], P(None, 'gx', 'gy', 'gz'), may hold values from -6 to 6
- current: float32 [32, 32, 16, 512], P(None, 'gx', 'gy', 'gz'), may hold values from -6 to 6
- eigvectors: bfloat16 [32, 16, 512, 512], P('gx', 'gy', 'gz'), may hold values from -0.125 to 0.125
- eigvalues: float32 [512], replicated, may hold values from 0.05 to 50
- reaction: float32 [32, 16, 512], P('gx', 'gy', 'gz'), may hold values from 0.25 to 4
Outputs:
- proposal: float32 [32, 32, 16, 512], P(None, 'gx', 'gy', 'gz')
All inputs are finite; a program needn't handle non-finite values.
Results may differ from a plain program's by a relative error of at most 0.00031.
Values sent between devices are 32-bit elements; how exact they have to be, the bound alone decides.
A program may use at most 64 MiB of HBM per device.

v0:
```python
import jax
import jax.numpy as jnp
from jax import lax
from jax.sharding import PartitionSpec as P

SWEEPS = 4


def with_halo(block, sides, width):
    for axis, dim in sides:
        count = lax.axis_size(axis)
        forward = [(i, i + 1) for i in range(count - 1)]
        backward = [(target, source) for source, target in forward]
        low = lax.ppermute(
            lax.slice_in_dim(block, block.shape[dim] - width, None, axis=dim), axis, forward
        )
        high = lax.ppermute(lax.slice_in_dim(block, 0, width, axis=dim), axis, backward)
        block = jnp.concatenate([low, block, high], axis=dim)
    return block


def prior_root(source, reaction):
    sweeps = SWEEPS
    diagonal = reaction + 6.0
    field = source / diagonal
    for sweep_index in range(sweeps - 1):
        padded = with_halo(field, (("gx", 1), ("gy", 2), ("gz", 3)), 1)
        total = padded[:, 2:, 1:-1, 1:-1] + padded[:, :-2, 1:-1, 1:-1]
        total = total + padded[:, 1:-1, 2:, 1:-1] + padded[:, 1:-1, :-2, 1:-1]
        total = total + padded[:, 1:-1, 1:-1, 2:] + padded[:, 1:-1, 1:-1, :-2]
        field = (source + total) / diagonal
    return field


def body(gradient, noise_draw, current, eigvectors, eigvalues, reaction):
    chains = gradient.shape[0]
    rank = eigvectors.shape[3]
    cells = reaction.shape[0] * reaction.shape[1] * reaction.shape[2]
    basis = eigvectors.reshape(cells, rank)
    stacked = jnp.concatenate(
        [gradient.reshape(chains, cells), noise_draw.reshape(chains, cells)], 0
    )
    partial_sums = jnp.dot(stacked, basis, preferred_element_type=jnp.float32)
    local_part = -0.5 * gradient.astype(jnp.float32) + 1.0 * noise_draw.astype(jnp.float32)
    sums = lax.psum(partial_sums, ("gx", "gy", "gz"))
    damp = eigvalues / (eigvalues + 1.0)
    root_damp = 1.0 - 1.0 / jnp.sqrt(1.0 + eigvalues)
    coef = (0.5 * damp * sums[:chains] - 1.0 * root_damp * sums[chains:]).astype(jnp.bfloat16)
    corr = lax.dot_general(
        coef, basis, (((1,), (1,)), ((), ())), preferred_element_type=jnp.float32
    )
    field = prior_root(local_part + corr.reshape(current.shape), reaction)
    return current + field


def solution(mesh):
    return jax.shard_map(
        body,
        mesh=mesh,
        in_specs=(
            P(None, "gx", "gy", "gz"),
            P(None, "gx", "gy", "gz"),
            P(None, "gx", "gy", "gz"),
            P("gx", "gy", "gz", None),
            P(),
            P("gx", "gy", "gz"),
        ),
        out_specs=P(None, "gx", "gy", "gz"),
        check_vma=False,
    )
```

profile of v0, /device:TPU:0, one launch (start us, length us, event | category | flops | bytes accessed | tf_op | source)
XLA Modules:
  0.0 262.8 jit_solution(8625238853567087662)
XLA Ops:
  6.5 1.9 copy_bitcast_fusion
  8.4 5.7 %fusion.22 = f32[64,512]{1,0:T(8,128)} fusion(bf16[8192,512]{1,0:T(8,128)(2,1)} %bitcast.18, bf16[32,8192]{1,0:T(8,128)(2,1)S(1)} %get-tuple-element.27, bf16[32,8192]{1,0:T(8,128)(2,1)S(1)} %get-tuple-element.28), kind=kOutput, calls=%fused_computation.80 | convolution fusion | flops 538968064 | bytes 9568256 | tf_op jit(solution)/shard_map/dot_general | solution.py:43
  14.2 127.2 %all-reduce.2.cloned.1.call-done = f32[64,512]{1,0:T(8,128)} async-done(((f32[64,512]{1,0:T(8,128)}), f32[64,512]{1,0:T(8,128)}) %all-reduce.2.cloned.1.call-update) | async-done | bytes 131088 | tf_op jit(solution)/shard_map/psum | solution.py:45
  141.5 6.0 %broadcast_divide_fusion = (f32[32,8,8,128]{3,0,2,1:T(8,128)S(1)}, f32[32,8,8,128]{3,0,2,1:T(8,128)S(1)}) fusion(f32[8,8,128]{2,1,0:T(8,128)S(1)} %broadcast_add_fusion, bf16[8,8,128,512]{3,2,1,0:T(8,128)(2,1)} %param.9, f32[64,512]{1,0:T(8,128)} %all-reduce.2.cloned.1.call-done, f32[512]{0:T(512)S(1)} %get-tuple-element.24, f32[512]{0:T(512)S(1)} %get-tuple-element.23, ...), kind=kOutput, calls=%fused_computation.86 | convolution fusion | flops 270073856 | bytes 11702272 | tf_op jit(solution)/shard_map/dot_general | solution.py:49
  147.5 3.4 %collective-permute-start.1 = (f32[32,1,8,128]{3,0,2,1:T(8,128)S(1)}, f32[32,1,8,128]{3,0,2,1:T(8,128)S(1)}, u32[]{:S(2)}, u32[]{:S(2)}) collective-permute-start(f32[32,1,8,128]{3,0,2,1:T(8,128)S(1)} %get-tuple-element.21), channel_id=1, source_target_pairs={{0,8},{8,16},{16,24},{1,9},{9,17},{17,25},{2,10},{10,18},{18,26},{... | collective-permute-start | bytes 393224 | tf_op jit(solution)/shard_map/ppermute | solution.py:14
  150.9 1.3 collective-permute-start
  153.4 4.7 %collective-permute-done = f32[32,1,8,128]{3,0,2,1:T(8,128)S(1)} collective-permute-done((f32[32,1,8,128]{3,0,2,1:T(8,128)S(1)}, f32[32,1,8,128]{3,0,2,1:T(8,128)S(1)}, u32[]{:S(2)}, u32[]{:S(2)}) %collective-permute-start) | collective-permute-done | bytes 131104 | tf_op jit(solution)/shard_map/ppermute | solution.py:17
  158.1 1.3 collective-permute-start.3
  159.5 1.3 collective-permute-start.2
  160.8 2.0 collective-permute-done.2
  163.4 2.3 fusion.37
  165.7 2.1 copy.13
  167.7 1.3 collective-permute-start.4
  169.0 2.1 copy.15
  171.1 4.6 %collective-permute-start.5 = (f32[32,10,10,1]{0,3,2,1:T(1,128)S(1)}, f32[32,10,10,1]{0,3,2,1:T(1,128)S(1)}, u32[]{:S(2)}, u32[]{:S(2)}) collective-permute-start(f32[32,10,10,1]{0,3,2,1:T(1,128)S(1)} %copy.15), channel_id=1, source_target_pairs={{0,1},{1,2},{2,3},{4,5},{5,6},{6,7},{8,9},{9,10},{10,11},{12,13},{... | collective-permute-start | bytes 38408 | tf_op jit(solution)/shard_map/ppermute | solution.py:14
  175.7 1.8 copy.14
  177.5 1.9 copy.16
  179.4 2.9 %fusion.17 = f32[32,8,8,128]{3,0,2,1:T(8,128)S(1)} fusion(f32[32,8,8,128]{3,0,2,1:T(8,128)S(1)} %get-tuple-element.26, f32[32,10,10,1]{3,0,2,1:T(8,128)} %copy.16, f32[32,10,1,128]{3,0,2,1:T(8,128)} %copy-done.5, f32[32,10,1,128]{3,0,2,1:T(8,128)} %copy-done.3, f32[32,1,8,128]{3,0,2,1:T(8,128)S(1)} %collective-permute-done, ...), kind=kLoop, calls=%fused_computation.58 | loop fusion | flops 6553600 | bytes 3793920 | tf_op jit(solution)/shard_map/div | solution.py:31
  182.3 3.9 %collective-permute-start.7 = (f32[32,1,8,128]{3,0,2,1:T(8,128)S(1)}, f32[32,1,8,128]{3,0,2,1:T(8,128)S(1)}, u32[]{:S(2)}, u32[]{:S(2)}) collective-permute-start(f32[32,1,8,128]{3,0,2,1:T(8,128)S(1)} %get-tuple-element.19), channel_id=1, source_target_pairs={{0,8},{8,16},{16,24},{1,9},{9,17},{17,25},{2,10},{10,18},{18,26},{... | collective-permute-start | bytes 393224 | tf_op jit(solution)/shard_map/ppermute | solution.py:14
  186.3 1.3 collective-permute-start.6
  188.8 4.4 %collective-permute-done.6 = f32[32,1,8,128]{3,0,2,1:T(8,128)S(1)} collective-permute-done((f32[32,1,8,128]{3,0,2,1:T(8,128)S(1)}, f32[32,1,8,128]{3,0,2,1:T(8,128)S(1)}, u32[]{:S(2)}, u32[]{:S(2)}) %collective-permute-start.6) | collective-permute-done | bytes 131104 | tf_op jit(solution)/shard_map/ppermute | solution.py:17
  193.2 1.3 collective-permute-start.9
  194.5 1.3 collective-permute-start.8
  195.8 2.0 collective-permute-done.8
  198.4 2.3 fusion.36
  200.7 2.1 copy.17
  202.7 1.3 collective-permute-start.10
  204.0 2.1 copy.19
  206.1 4.8 %collective-permute-start.11 = (f32[32,10,10,1]{0,3,2,1:T(1,128)S(1)}, f32[32,10,10,1]{0,3,2,1:T(1,128)S(1)}, u32[]{:S(2)}, u32[]{:S(2)}) collective-permute-start(f32[32,10,10,1]{0,3,2,1:T(1,128)S(1)} %copy.19), channel_id=1, source_target_pairs={{0,1},{1,2},{2,3},{4,5},{5,6},{6,7},{8,9},{9,10},{10,11},{12,13},{... | collective-permute-start | bytes 38408 | tf_op jit(solution)/shard_map/ppermute | solution.py:14
  210.9 1.8 copy.18
  212.8 1.9 copy.20
  214.6 2.9 %fusion.10 = f32[32,8,8,128]{3,0,2,1:T(8,128)S(1)} fusion(f32[32,8,8,128]{3,0,2,1:T(8,128)S(1)} %get-tuple-element.26, f32[32,10,10,1]{3,0,2,1:T(8,128)} %copy.20, f32[32,10,1,128]{3,0,2,1:T(8,128)} %copy-done.6, f32[32,10,1,128]{3,0,2,1:T(8,128)} %copy-done.4, f32[32,1,8,128]{3,0,2,1:T(8,128)S(1)} %collective-permute-done.6, ...), kind=kLoop, calls=%fused_computation.33 | loop fusion | flops 6553600 | bytes 3793920 | tf_op jit(solution)/shard_map/div | solution.py:31
  217.5 3.4 %collective-permute-start.13 = (f32[32,1,8,128]{3,0,2,1:T(8,128)S(1)}, f32[32,1,8,128]{3,0,2,1:T(8,128)S(1)}, u32[]{:S(2)}, u32[]{:S(2)}) collective-permute-start(f32[32,1,8,128]{3,0,2,1:T(8,128)S(1)} %get-tuple-element.17), channel_id=1, source_target_pairs={{0,8},{8,16},{16,24},{1,9},{9,17},{17,25},{2,10},{10,18},{18,26},{... | collective-permute-start | bytes 393224 | tf_op jit(solution)/shard_map/ppermute | solution.py:14
  220.9 1.3 collective-permute-start.12
  222.2 1.5 collective-permute-done.13
  223.7 4.1 %collective-permute-done.12 = f32[32,1,8,128]{3,0,2,1:T(8,128)S(1)} collective-permute-done((f32[32,1,8,128]{3,0,2,1:T(8,128)S(1)}, f32[32,1,8,128]{3,0,2,1:T(8,128)S(1)}, u32[]{:S(2)}, u32[]{:S(2)}) %collective-permute-start.12) | collective-permute-done | bytes 131104 | tf_op jit(solution)/shard_map/ppermute | solution.py:17
  227.8 1.3 collective-permute-start.15
  229.1 1.3 collective-permute-start.14
  230.5 2.0 collective-permute-done.14
  233.1 2.2 fusion.35
  235.3 2.1 copy.21
  237.4 1.3 collective-permute-start.16
  238.7 2.7 %copy.23 = f32[32,10,10,1]{0,3,2,1:T(1,128)} copy(f32[32,10,10,1]{3,0,2,1:T(8,128)} %get-tuple-element.6) | data formatting | bytes 25600 | tf_op jit(solution)/shard_map/slice | solution.py:15
  241.4 5.5 %collective-permute-start.17 = (f32[32,10,10,1]{0,3,2,1:T(1,128)}, f32[32,10,10,1]{0,3,2,1:T(1,128)}, u32[]{:S(2)}, u32[]{:S(2)}) collective-permute-start(f32[32,10,10,1]{0,3,2,1:T(1,128)} %copy.23), channel_id=1, source_target_pairs={{0,1},{1,2},{2,3},{4,5},{5,6},{6,7},{8,9},{9,10},{10,11},{12,13},{... | collective-permute-start | bytes 38408 | tf_op jit(solution)/shard_map/ppermute | solution.py:14
  246.9 1.9 copy.22
  248.8 2.6 %copy.24 = f32[32,10,10,1]{3,0,2,1:T(8,128)} copy(f32[32,10,10,1]{0,3,2,1:T(1,128)} %collective-permute-done.17) | data formatting | bytes 25600 | tf_op jit(solution)/shard_map/ppermute | solution.py:14
  251.4 3.0 %fusion.3 = f32[32,8,8,128]{3,0,2,1:T(8,128)S(1)} fusion(f32[32,8,8,128]{3,0,2,1:T(8,128)S(1)} %get-tuple-element.26, f32[32,10,10,1]{3,0,2,1:T(8,128)} %copy.24, f32[32,10,1,128]{3,0,2,1:T(8,128)} %copy-done.8, f32[32,10,1,128]{3,0,2,1:T(8,128)} %copy-done.7, f32[32,1,8,128]{3,0,2,1:T(8,128)S(1)} %collective-permute-done.12, ...), kind=kLoop, calls=%fused_computation.8 | loop fusion | flops 6815744 | bytes 4842496 | tf_op jit(solution)/shard_map/add | solution.py:53
  254.4 1.6 copy.26
  (46 shorter events, 4.6 us)
Async XLA Ops:
  6.5 134.9 %all-reduce.2.cloned.1.call-start = ((), (), s32[]{:S(2)}) async-start(), calls=%async_computation | async-start | bytes 262144 | tf_op jit(solution)/shard_map/psum | solution.py:45
  8.4 5.8 %copy-start.9 = (f32[8,8,128]{2,1,0:T(8,128)S(1)}, f32[8,8,128]{2,1,0:T(8,128)}, u32[]{:S(2)}) copy-start(f32[8,8,128]{2,1,0:T(8,128)} %param.11) | copy-start | bytes 98308
  8.4 5.8 %copy-start.10 = (f32[512]{0:T(512)S(1)}, f32[512]{0:T(512)}, u32[]{:S(2)}) copy-start(f32[512]{0:T(512)} %param.10) | copy-start | bytes 6148
  8.4 133.0 %copy-start = (bf16[32,8,8,128]{3,2,1,0:T(8,128)(2,1)S(1)}, bf16[32,8,8,128]{3,2,1,0:T(8,128)(2,1)}, u32[]{:S(2)}) copy-start(bf16[32,8,8,128]{3,2,1,0:T(8,128)(2,1)} %param.7) | copy-start | bytes 1572868
  8.4 133.0 %copy-start.1 = (bf16[32,8,8,128]{3,2,1,0:T(8,128)(2,1)S(1)}, bf16[32,8,8,128]{3,2,1,0:T(8,128)(2,1)}, u32[]{:S(2)}) copy-start(bf16[32,8,8,128]{3,2,1,0:T(8,128)(2,1)} %param.6) | copy-start | bytes 1572868
  147.5 5.9 %collective-permute-start.1 = (f32[32,1,8,128]{3,0,2,1:T(8,128)S(1)}, f32[32,1,8,128]{3,0,2,1:T(8,128)S(1)}, u32[]{:S(2)}, u32[]{:S(2)}) collective-permute-start(f32[32,1,8,128]{3,0,2,1:T(8,128)S(1)} %get-tuple-element.21), channel_id=1, source_target_pairs={{0,8},{8,16},{16,24},{1,9},{9,17},{17,25},{2,10},{10,18},{18,26},{... | collective-permute-start | bytes 393224 | tf_op jit(solution)/shard_map/ppermute | solution.py:14
  150.9 7.2 %collective-permute-start = (f32[32,1,8,128]{3,0,2,1:T(8,128)S(1)}, f32[32,1,8,128]{3,0,2,1:T(8,128)S(1)}, u32[]{:S(2)}, u32[]{:S(2)}) collective-permute-start(f32[32,1,8,128]{3,0,2,1:T(8,128)S(1)} %get-tuple-element.22), channel_id=1, source_target_pairs={{8,0},{16,8},{24,16},{9,1},{17,9},{25,17},{10,2},{18,10},{26,18},{... | collective-permute-start | bytes 393224 | tf_op jit(solution)/shard_map/ppermute | solution.py:17
  158.1 2.6 collective-permute-start.3
  159.5 3.3 %collective-permute-start.2 = (f32[32,10,1,128]{3,0,2,1:T(8,128)S(1)}, f32[32,10,1,128]{3,0,2,1:T(8,128)S(1)}, u32[]{:S(2)}, u32[]{:S(2)}) collective-permute-start(f32[32,10,1,128]{3,0,2,1:T(8,128)S(1)} %get-tuple-element.16), channel_id=1, source_target_pairs={{4,0},{5,1},{6,2},{7,3},{12,8},{13,9},{14,10},{15,11},{20,16},{21,... | collective-permute-start | bytes 491528 | tf_op jit(solution)/shard_map/ppermute | solution.py:17
  160.8 2.2 copy-start.3
  162.7 0.7 copy-start.5
  167.7 7.9 %collective-permute-start.4 = (f32[32,10,10,1]{0,3,2,1:T(1,128)S(1)}, f32[32,10,10,1]{0,3,2,1:T(1,128)S(1)}, u32[]{:S(2)}, u32[]{:S(2)}) collective-permute-start(f32[32,10,10,1]{0,3,2,1:T(1,128)S(1)} %copy.13), channel_id=1, source_target_pairs={{1,0},{2,1},{3,2},{5,4},{6,5},{7,6},{9,8},{10,9},{11,10},{13,12},{... | collective-permute-start | bytes 38408 | tf_op jit(solution)/shard_map/ppermute | solution.py:17
  171.1 6.4 %collective-permute-start.5 = (f32[32,10,10,1]{0,3,2,1:T(1,128)S(1)}, f32[32,10,10,1]{0,3,2,1:T(1,128)S(1)}, u32[]{:S(2)}, u32[]{:S(2)}) collective-permute-start(f32[32,10,10,1]{0,3,2,1:T(1,128)S(1)} %copy.15), channel_id=1, source_target_pairs={{0,1},{1,2},{2,3},{4,5},{5,6},{6,7},{8,9},{9,10},{10,11},{12,13},{... | collective-permute-start | bytes 38408 | tf_op jit(solution)/shard_map/ppermute | solution.py:14
  182.3 6.4 %collective-permute-start.7 = (f32[32,1,8,128]{3,0,2,1:T(8,128)S(1)}, f32[32,1,8,128]{3,0,2,1:T(8,128)S(1)}, u32[]{:S(2)}, u32[]{:S(2)}) collective-permute-start(f32[32,1,8,128]{3,0,2,1:T(8,128)S(1)} %get-tuple-element.19), channel_id=1, source_target_pairs={{0,8},{8,16},{16,24},{1,9},{9,17},{17,25},{2,10},{10,18},{18,26},{... | collective-permute-start | bytes 393224 | tf_op jit(solution)/shard_map/ppermute | solution.py:14
  186.3 6.9 %collective-permute-start.6 = (f32[32,1,8,128]{3,0,2,1:T(8,128)S(1)}, f32[32,1,8,128]{3,0,2,1:T(8,128)S(1)}, u32[]{:S(2)}, u32[]{:S(2)}) collective-permute-start(f32[32,1,8,128]{3,0,2,1:T(8,128)S(1)} %get-tuple-element.20), channel_id=1, source_target_pairs={{8,0},{16,8},{24,16},{9,1},{17,9},{25,17},{10,2},{18,10},{26,18},{... | collective-permute-start | bytes 393224 | tf_op jit(solution)/shard_map/ppermute | solution.py:17
  193.2 2.6 collective-permute-start.9
  194.5 3.3 %collective-permute-start.8 = (f32[32,10,1,128]{3,0,2,1:T(8,128)S(1)}, f32[32,10,1,128]{3,0,2,1:T(8,128)S(1)}, u32[]{:S(2)}, u32[]{:S(2)}) collective-permute-start(f32[32,10,1,128]{3,0,2,1:T(8,128)S(1)} %get-tuple-element.14), channel_id=1, source_target_pairs={{4,0},{5,1},{6,2},{7,3},{12,8},{13,9},{14,10},{15,11},{20,16},{21,... | collective-permute-start | bytes 491528 | tf_op jit(solution)/shard_map/ppermute | solution.py:17
  195.8 2.2 copy-start.4
  197.8 0.7 copy-start.6
  202.7 8.2 %collective-permute-start.10 = (f32[32,10,10,1]{0,3,2,1:T(1,128)S(1)}, f32[32,10,10,1]{0,3,2,1:T(1,128)S(1)}, u32[]{:S(2)}, u32[]{:S(2)}) collective-permute-start(f32[32,10,10,1]{0,3,2,1:T(1,128)S(1)} %copy.17), channel_id=1, source_target_pairs={{1,0},{2,1},{3,2},{5,4},{6,5},{7,6},{9,8},{10,9},{11,10},{13,12},{... | collective-permute-start | bytes 38408 | tf_op jit(solution)/shard_map/ppermute | solution.py:17
  206.1 6.6 %collective-permute-start.11 = (f32[32,10,10,1]{0,3,2,1:T(1,128)S(1)}, f32[32,10,10,1]{0,3,2,1:T(1,128)S(1)}, u32[]{:S(2)}, u32[]{:S(2)}) collective-permute-start(f32[32,10,10,1]{0,3,2,1:T(1,128)S(1)} %copy.19), channel_id=1, source_target_pairs={{0,1},{1,2},{2,3},{4,5},{5,6},{6,7},{8,9},{9,10},{10,11},{12,13},{... | collective-permute-start | bytes 38408 | tf_op jit(solution)/shard_map/ppermute | solution.py:14
  217.5 6.1 %collective-permute-start.13 = (f32[32,1,8,128]{3,0,2,1:T(8,128)S(1)}, f32[32,1,8,128]{3,0,2,1:T(8,128)S(1)}, u32[]{:S(2)}, u32[]{:S(2)}) collective-permute-start(f32[32,1,8,128]{3,0,2,1:T(8,128)S(1)} %get-tuple-element.17), channel_id=1, source_target_pairs={{0,8},{8,16},{16,24},{1,9},{9,17},{17,25},{2,10},{10,18},{18,26},{... | collective-permute-start | bytes 393224 | tf_op jit(solution)/shard_map/ppermute | solution.py:14
  220.9 6.9 %collective-permute-start.12 = (f32[32,1,8,128]{3,0,2,1:T(8,128)S(1)}, f32[32,1,8,128]{3,0,2,1:T(8,128)S(1)}, u32[]{:S(2)}, u32[]{:S(2)}) collective-permute-start(f32[32,1,8,128]{3,0,2,1:T(8,128)S(1)} %get-tuple-element.18), channel_id=1, source_target_pairs={{8,0},{16,8},{24,16},{9,1},{17,9},{25,17},{10,2},{18,10},{26,18},{... | collective-permute-start | bytes 393224 | tf_op jit(solution)/shard_map/ppermute | solution.py:17
  227.8 2.6 collective-permute-start.15
  229.1 3.3 %collective-permute-start.14 = (f32[32,10,1,128]{3,0,2,1:T(8,128)S(1)}, f32[32,10,1,128]{3,0,2,1:T(8,128)S(1)}, u32[]{:S(2)}, u32[]{:S(2)}) collective-permute-start(f32[32,10,1,128]{3,0,2,1:T(8,128)S(1)} %get-tuple-element.12), channel_id=1, source_target_pairs={{4,0},{5,1},{6,2},{7,3},{12,8},{13,9},{14,10},{15,11},{20,16},{21,... | collective-permute-start | bytes 491528 | tf_op jit(solution)/shard_map/ppermute | solution.py:17
  230.4 2.2 copy-start.7
  232.4 0.7 copy-start.8
  237.4 9.5 %collective-permute-start.16 = (f32[32,10,10,1]{0,3,2,1:T(1,128)S(1)}, f32[32,10,10,1]{0,3,2,1:T(1,128)S(1)}, u32[]{:S(2)}, u32[]{:S(2)}) collective-permute-start(f32[32,10,10,1]{0,3,2,1:T(1,128)S(1)} %copy.21), channel_id=1, source_target_pairs={{1,0},{2,1},{3,2},{5,4},{6,5},{7,6},{9,8},{10,9},{11,10},{13,12},{... | collective-permute-start | bytes 38408 | tf_op jit(solution)/shard_map/ppermute | solution.py:17
  241.4 10.0 %copy-start.2 = (f32[32,8,8,128]{3,2,1,0:T(8,128)S(1)}, f32[32,8,8,128]{3,2,1,0:T(8,128)}, u32[]{:S(2)}) copy-start(f32[32,8,8,128]{3,2,1,0:T(8,128)} %param.8) | copy-start | bytes 3145732
  241.4 7.4 %collective-permute-start.17 = (f32[32,10,10,1]{0,3,2,1:T(1,128)}, f32[32,10,10,1]{0,3,2,1:T(1,128)}, u32[]{:S(2)}, u32[]{:S(2)}) collective-permute-start(f32[32,10,10,1]{0,3,2,1:T(1,128)} %copy.23), channel_id=1, source_target_pairs={{0,1},{1,2},{2,3},{4,5},{5,6},{6,7},{8,9},{9,10},{10,11},{12,13},{... | collective-permute-start | bytes 38408 | tf_op jit(solution)/shard_map/ppermute | solution.py:14
Sparse Core Ops, SparseCore 0:
  14.3 127.1 all-reduce.1
where the time goes:
time: 264 us; the launch traced here: 263 us
  waiting for transfers between devices  150 us (57%)
  starting transfers between devices  41.1 us (16%)
  local copies, waits for them, and re-layouts  36.7 us (14%)
  between operations  13.8 us (5%)
  matrix products  11.7 us (4%)
  other arithmetic  9.37 us (4%)
    psum x1, waiting for transfers between devices, body(): sums = lax.psum(partial_sums, ('gx', 'gy', 'gz'))  127 us
    ppermute x9, starting transfers between devices, with_halo(): lax.ppermute(lax.slice_in_dim(block, block.shape[dim] - width, None, axis...  29.4 us
    ppermute x9, waiting for transfers between devices, with_halo(): lax.ppermute(lax.slice_in_dim(block, 0, width, axis=dim), axis, backward)  19.1 us
    slice x6, local copies, waits for them, and re-layouts, with_halo(): lax.slice_in_dim(block, 0, width, axis=dim)  13 us
    ppermute x9, starting transfers between devices, with_halo(): lax.ppermute(lax.slice_in_dim(block, 0, width, axis=dim), axis, backward)  11.6 us
    slice x6, local copies, waits for them, and re-layouts, with_halo(): lax.slice_in_dim(block, block.shape[dim] - width, None, axis=dim)  6.9 us
    ppermute x3, local copies, waits for them, and re-layouts, with_halo(): lax.ppermute(lax.slice_in_dim(block, block.shape[dim] - width, None, axis...  6.34 us
    dot_general x1, matrix products, body(): lax.dot_general(coef, basis, (((1,), (1,)), ((), ())), preferred_element_...  6.04 us
  transfers between devices with their start and end apart: 19, of which 10 were waited for; matrix products, arithmetic and copies ran while one was open for 5% of the time, Pallas kernels for 0%

commit v1 on v0

--- a/solution.py
+++ b/solution.py
@@ -42,7 +42,7 @@
     )
     partial_sums = jnp.dot(stacked, basis, preferred_element_type=jnp.float32)
     local_part = -0.5 * gradient.astype(jnp.float32) + 1.0 * noise_draw.astype(jnp.float32)
-    sums = lax.psum(partial_sums, ("gx", "gy", "gz"))
+    sums = lax.psum(lax.psum(partial_sums, ("gy", "gz")), "gx")
     damp = eigvalues / (eigvalues + 1.0)
     root_damp = 1.0 - 1.0 / jnp.sqrt(1.0 + eigvalues)
     coef = (0.5 * damp * sums[:chains] - 1.0 * root_damp * sums[chains:]).astype(jnp.bfloat16)

time: 264 us -> 238 us (0.902)
  waiting for transfers between devices: 150 us -> 125 us
    psum x1 -> x2, waiting for transfers between devices: 127 us -> 102 us  [body(): sums = lax.psum(lax.psum(partial_sums, ('gy', 'gz')), 'gx')]
  transfers between devices with their start and end apart: 19 -> 20, of which waited for: 10 -> 11; matrix products, arithmetic and copies ran while one was open for 5% -> 5% of each run, Pallas kernels for 0% -> 0%
where the time goes in v1:
time: 238 us; the launch traced here: 237 us
  waiting for transfers between devices  125 us (53%)
  starting transfers between devices  40.5 us (17%)
  local copies, waits for them, and re-layouts  36.8 us (15%)
  between operations  13.8 us (6%)
  matrix products  11.7 us (5%)
  other arithmetic  9.38 us (4%)
    psum x2, waiting for transfers between devices, body(): sums = lax.psum(lax.psum(partial_sums, ('gy', 'gz')), 'gx')  102 us
    ppermute x9, starting transfers between devices, with_halo(): lax.ppermute(lax.slice_in_dim(block, block.shape[dim] - width, None, axis...  28.9 us
    ppermute x9, waiting for transfers between devices, with_halo(): lax.ppermute(lax.slice_in_dim(block, 0, width, axis=dim), axis, backward)  19 us
    slice x6, local copies, waits for them, and re-layouts, with_halo(): lax.slice_in_dim(block, 0, width, axis=dim)  13 us
    ppermute x9, starting transfers between devices, with_halo(): lax.ppermute(lax.slice_in_dim(block, 0, width, axis=dim), axis, backward)  11.6 us
    slice x6, local copies, waits for them, and re-layouts, with_halo(): lax.slice_in_dim(block, block.shape[dim] - width, None, axis=dim)  6.9 us
    ppermute x3, local copies, waits for them, and re-layouts, with_halo(): lax.ppermute(lax.slice_in_dim(block, block.shape[dim] - width, None, axis...  6.34 us
    dot_general x1, matrix products, body(): lax.dot_general(coef, basis, (((1,), (1,)), ((), ())), preferred_element_...  6.05 us
  transfers between devices with their start and end apart: 20, of which 11 were waited for; matrix products, arithmetic and copies ran while one was open for 5% of the time, Pallas kernels for 0%

profile of v1, /device:TPU:0, one launch (start us, length us, event | category | flops | bytes accessed | tf_op | source)
XLA Modules:
  0.0 237.1 jit_solution(12538210373431239612)
XLA Ops:
  6.5 1.9 copy_bitcast_fusion
  8.4 5.7 %fusion.22 = f32[64,512]{1,0:T(8,128)} fusion(bf16[8192,512]{1,0:T(8,128)(2,1)} %bitcast.18, bf16[32,8192]{1,0:T(8,128)(2,1)S(1)} %get-tuple-element.27, bf16[32,8192]{1,0:T(8,128)(2,1)S(1)} %get-tuple-element.28), kind=kOutput, calls=%fused_computation.80 | convolution fusion | flops 538968064 | bytes 9568256 | tf_op jit(solution)/shard_map/dot_general | solution.py:43
  14.2 57.8 %all-reduce.3.cloned.1.call-done = f32[64,512]{1,0:T(8,128)} async-done(((f32[64,512]{1,0:T(8,128)}), f32[64,512]{1,0:T(8,128)}) %all-reduce.3.cloned.1.call-update) | async-done | bytes 131088 | tf_op jit(solution)/shard_map/psum | solution.py:45
  72.1 44.1 %all-reduce.5.cloned.1.call-done = f32[64,512]{1,0:T(8,128)} async-done(((f32[64,512]{1,0:T(8,128)}), f32[64,512]{1,0:T(8,128)}) %all-reduce.5.cloned.1.call-update) | async-done | bytes 131088 | tf_op jit(solution)/shard_map/psum | solution.py:45
  116.2 6.0 %broadcast_divide_fusion = (f32[32,8,8,128]{3,0,2,1:T(8,128)S(1)}, f32[32,8,8,128]{3,0,2,1:T(8,128)S(1)}) fusion(f32[8,8,128]{2,1,0:T(8,128)S(1)} %broadcast_add_fusion, bf16[8,8,128,512]{3,2,1,0:T(8,128)(2,1)} %param.9, f32[64,512]{1,0:T(8,128)} %all-reduce.5.cloned.1.call-done, f32[512]{0:T(512)S(1)} %get-tuple-element.24, f32[512]{0:T(512)S(1)} %get-tuple-element.23, ...), kind=kOutput, calls=%fused_computation.86 | convolution fusion | flops 270073856 | bytes 11702272 | tf_op jit(solution)/shard_map/dot_general | solution.py:49
  122.3 3.4 %collective-permute-start.1 = (f32[32,1,8,128]{3,0,2,1:T(8,128)S(1)}, f32[32,1,8,128]{3,0,2,1:T(8,128)S(1)}, u32[]{:S(2)}, u32[]{:S(2)}) collective-permute-start(f32[32,1,8,128]{3,0,2,1:T(8,128)S(1)} %get-tuple-element.21), channel_id=1, source_target_pairs={{0,8},{8,16},{16,24},{1,9},{9,17},{17,25},{2,10},{10,18},{18,26},{... | collective-permute-start | bytes 393224 | tf_op jit(solution)/shard_map/ppermute | solution.py:14
  125.7 1.3 collective-permute-start
  128.2 4.6 %collective-permute-done = f32[32,1,8,128]{3,0,2,1:T(8,128)S(1)} collective-permute-done((f32[32,1,8,128]{3,0,2,1:T(8,128)S(1)}, f32[32,1,8,128]{3,0,2,1:T(8,128)S(1)}, u32[]{:S(2)}, u32[]{:S(2)}) %collective-permute-start) | collective-permute-done | bytes 131104 | tf_op jit(solution)/shard_map/ppermute | solution.py:17
  132.8 1.3 collective-permute-start.3
  134.1 1.3 collective-permute-start.2
  135.5 2.0 collective-permute-done.2
  138.1 2.3 fusion.37
  140.3 2.1 copy.13
  142.4 1.3 collective-permute-start.4
  143.7 2.1 copy.15
  145.8 4.6 %collective-permute-start.5 = (f32[32,10,10,1]{0,3,2,1:T(1,128)S(1)}, f32[32,10,10,1]{0,3,2,1:T(1,128)S(1)}, u32[]{:S(2)}, u32[]{:S(2)}) collective-permute-start(f32[32,10,10,1]{0,3,2,1:T(1,128)S(1)} %copy.15), channel_id=1, source_target_pairs={{0,1},{1,2},{2,3},{4,5},{5,6},{6,7},{8,9},{9,10},{10,11},{12,13},{... | collective-permute-start | bytes 38408 | tf_op jit(solution)/shard_map/ppermute | solution.py:14
  150.4 1.8 copy.14
  152.2 1.9 copy.16
  154.1 2.9 %fusion.17 = f32[32,8,8,128]{3,0,2,1:T(8,128)S(1)} fusion(f32[32,8,8,128]{3,0,2,1:T(8,128)S(1)} %get-tuple-element.26, f32[32,10,10,1]{3,0,2,1:T(8,128)} %copy.16, f32[32,10,1,128]{3,0,2,1:T(8,128)} %copy-done.5, f32[32,10,1,128]{3,0,2,1:T(8,128)} %copy-done.3, f32[32,1,8,128]{3,0,2,1:T(8,128)S(1)} %collective-permute-done, ...), kind=kLoop, calls=%fused_computation.58 | loop fusion | flops 6553600 | bytes 3793920 | tf_op jit(solution)/shard_map/div | solution.py:31
  157.0 3.9 %collective-permute-start.7 = (f32[32,1,8,128]{3,0,2,1:T(8,128)S(1)}, f32[32,1,8,128]{3,0,2,1:T(8,128)S(1)}, u32[]{:S(2)}, u32[]{:S(2)}) collective-permute-start(f32[32,1,8,128]{3,0,2,1:T(8,128)S(1)} %get-tuple-element.19), channel_id=1, source_target_pairs={{0,8},{8,16},{16,24},{1,9},{9,17},{17,25},{2,10},{10,18},{18,26},{... | collective-permute-start | bytes 393224 | tf_op jit(solution)/shard_map/ppermute | solution.py:14
  160.9 1.3 collective-permute-start.6
  163.4 4.4 %collective-permute-done.6 = f32[32,1,8,128]{3,0,2,1:T(8,128)S(1)} collective-permute-done((f32[32,1,8,128]{3,0,2,1:T(8,128)S(1)}, f32[32,1,8,128]{3,0,2,1:T(8,128)S(1)}, u32[]{:S(2)}, u32[]{:S(2)}) %collective-permute-start.6) | collective-permute-done | bytes 131104 | tf_op jit(solution)/shard_map/ppermute | solution.py:17
  167.8 1.3 collective-permute-start.9
  169.1 1.3 collective-permute-start.8
  170.5 2.0 collective-permute-done.8
  173.3 2.3 fusion.36
  175.5 2.1 copy.17
  177.6 1.3 collective-permute-start.10
  178.9 2.1 copy.19
  181.0 4.8 %collective-permute-start.11 = (f32[32,10,10,1]{0,3,2,1:T(1,128)S(1)}, f32[32,10,10,1]{0,3,2,1:T(1,128)S(1)}, u32[]{:S(2)}, u32[]{:S(2)}) collective-permute-start(f32[32,10,10,1]{0,3,2,1:T(1,128)S(1)} %copy.19), channel_id=1, source_target_pairs={{0,1},{1,2},{2,3},{4,5},{5,6},{6,7},{8,9},{9,10},{10,11},{12,13},{... | collective-permute-start | bytes 38408 | tf_op jit(solution)/shard_map/ppermute | solution.py:14
  185.8 1.8 copy.18
  187.6 1.9 copy.20
  189.5 2.9 %fusion.10 = f32[32,8,8,128]{3,0,2,1:T(8,128)S(1)} fusion(f32[32,8,8,128]{3,0,2,1:T(8,128)S(1)} %get-tuple-element.26, f32[32,10,10,1]{3,0,2,1:T(8,128)} %copy.20, f32[32,10,1,128]{3,0,2,1:T(8,128)} %copy-done.6, f32[32,10,1,128]{3,0,2,1:T(8,128)} %copy-done.4, f32[32,1,8,128]{3,0,2,1:T(8,128)S(1)} %collective-permute-done.6, ...), kind=kLoop, calls=%fused_computation.33 | loop fusion | flops 6553600 | bytes 3793920 | tf_op jit(solution)/shard_map/div | solution.py:31
  192.4 2.8 %collective-permute-start.13 = (f32[32,1,8,128]{3,0,2,1:T(8,128)S(1)}, f32[32,1,8,128]{3,0,2,1:T(8,128)S(1)}, u32[]{:S(2)}, u32[]{:S(2)}) collective-permute-start(f32[32,1,8,128]{3,0,2,1:T(8,128)S(1)} %get-tuple-element.17), channel_id=1, source_target_pairs={{0,8},{8,16},{16,24},{1,9},{9,17},{17,25},{2,10},{10,18},{18,26},{... | collective-permute-start | bytes 393224 | tf_op jit(solution)/shard_map/ppermute | solution.py:14
  196.5 1.5 collective-permute-done.13
  198.0 4.1 %collective-permute-done.12 = f32[32,1,8,128]{3,0,2,1:T(8,128)S(1)} collective-permute-done((f32[32,1,8,128]{3,0,2,1:T(8,128)S(1)}, f32[32,1,8,128]{3,0,2,1:T(8,128)S(1)}, u32[]{:S(2)}, u32[]{:S(2)}) %collective-permute-start.12) | collective-permute-done | bytes 131104 | tf_op jit(solution)/shard_map/ppermute | solution.py:17
  202.2 1.3 collective-permute-start.15
  203.5 1.3 collective-permute-start.14
  204.8 2.0 collective-permute-done.14
  207.4 2.2 fusion.35
  209.7 2.1 copy.21
  211.7 1.3 collective-permute-start.16
  213.0 2.7 %copy.23 = f32[32,10,10,1]{0,3,2,1:T(1,128)} copy(f32[32,10,10,1]{3,0,2,1:T(8,128)} %get-tuple-element.6) | data formatting | bytes 25600 | tf_op jit(solution)/shard_map/slice | solution.py:15
  215.7 5.5 %collective-permute-start.17 = (f32[32,10,10,1]{0,3,2,1:T(1,128)}, f32[32,10,10,1]{0,3,2,1:T(1,128)}, u32[]{:S(2)}, u32[]{:S(2)}) collective-permute-start(f32[32,10,10,1]{0,3,2,1:T(1,128)} %copy.23), channel_id=1, source_target_pairs={{0,1},{1,2},{2,3},{4,5},{5,6},{6,7},{8,9},{9,10},{10,11},{12,13},{... | collective-permute-start | bytes 38408 | tf_op jit(solution)/shard_map/ppermute | solution.py:14
  221.2 1.9 copy.22
  223.1 2.6 %copy.24 = f32[32,10,10,1]{3,0,2,1:T(8,128)} copy(f32[32,10,10,1]{0,3,2,1:T(1,128)} %collective-permute-done.17) | data formatting | bytes 25600 | tf_op jit(solution)/shard_map/ppermute | solution.py:14
  225.7 3.0 %fusion.3 = f32[32,8,8,128]{3,0,2,1:T(8,128)S(1)} fusion(f32[32,8,8,128]{3,0,2,1:T(8,128)S(1)} %get-tuple-element.26, f32[32,10,10,1]{3,0,2,1:T(8,128)} %copy.24, f32[32,10,1,128]{3,0,2,1:T(8,128)} %copy-done.8, f32[32,10,1,128]{3,0,2,1:T(8,128)} %copy-done.7, f32[32,1,8,128]{3,0,2,1:T(8,128)S(1)} %collective-permute-done.12, ...), kind=kLoop, calls=%fused_computation.8 | loop fusion | flops 6815744 | bytes 4842496 | tf_op jit(solution)/shard_map/add | solution.py:53
  228.7 1.6 copy.26
  (49 shorter events, 6.1 us)
Async XLA Ops:
  6.5 65.5 %all-reduce.3.cloned.1.call-start = ((), (), s32[]{:S(2)}) async-start(), calls=%async_computation | async-start | bytes 262144 | tf_op jit(solution)/shard_map/psum | solution.py:45
  8.4 5.8 %copy-start.9 = (f32[8,8,128]{2,1,0:T(8,128)S(1)}, f32[8,8,128]{2,1,0:T(8,128)}, u32[]{:S(2)}) copy-start(f32[8,8,128]{2,1,0:T(8,128)} %param.11) | copy-start | bytes 98308
  8.4 63.6 %copy-start.10 = (f32[512]{0:T(512)S(1)}, f32[512]{0:T(512)}, u32[]{:S(2)}) copy-start(f32[512]{0:T(512)} %param.10) | copy-start | bytes 6148
  8.4 107.8 %copy-start = (bf16[32,8,8,128]{3,2,1,0:T(8,128)(2,1)S(1)}, bf16[32,8,8,128]{3,2,1,0:T(8,128)(2,1)}, u32[]{:S(2)}) copy-start(bf16[32,8,8,128]{3,2,1,0:T(8,128)(2,1)} %param.7) | copy-start | bytes 1572868
  8.4 107.8 %copy-start.1 = (bf16[32,8,8,128]{3,2,1,0:T(8,128)(2,1)S(1)}, bf16[32,8,8,128]{3,2,1,0:T(8,128)(2,1)}, u32[]{:S(2)}) copy-start(bf16[32,8,8,128]{3,2,1,0:T(8,128)(2,1)} %param.6) | copy-start | bytes 1572868
  14.2 102.0 %all-reduce.5.cloned.1.call-start = ((), (), s32[]{:S(2)}) async-start(), calls=%async_computation.1 | async-start | bytes 262144 | tf_op jit(solution)/shard_map/psum | solution.py:45
  122.3 5.9 %collective-permute-start.1 = (f32[32,1,8,128]{3,0,2,1:T(8,128)S(1)}, f32[32,1,8,128]{3,0,2,1:T(8,128)S(1)}, u32[]{:S(2)}, u32[]{:S(2)}) collective-permute-start(f32[32,1,8,128]{3,0,2,1:T(8,128)S(1)} %get-tuple-element.21), channel_id=1, source_target_pairs={{0,8},{8,16},{16,24},{1,9},{9,17},{17,25},{2,10},{10,18},{18,26},{... | collective-permute-start | bytes 393224 | tf_op jit(solution)/shard_map/ppermute | solution.py:14
  125.7 7.1 %collective-permute-start = (f32[32,1,8,128]{3,0,2,1:T(8,128)S(1)}, f32[32,1,8,128]{3,0,2,1:T(8,128)S(1)}, u32[]{:S(2)}, u32[]{:S(2)}) collective-permute-start(f32[32,1,8,128]{3,0,2,1:T(8,128)S(1)} %get-tuple-element.22), channel_id=1, source_target_pairs={{8,0},{16,8},{24,16},{9,1},{17,9},{25,17},{10,2},{18,10},{26,18},{... | collective-permute-start | bytes 393224 | tf_op jit(solution)/shard_map/ppermute | solution.py:17
  132.8 2.6 %collective-permute-start.3 = (f32[32,10,1,128]{3,0,2,1:T(8,128)S(1)}, f32[32,10,1,128]{3,0,2,1:T(8,128)S(1)}, u32[]{:S(2)}, u32[]{:S(2)}) collective-permute-start(f32[32,10,1,128]{3,0,2,1:T(8,128)S(1)} %get-tuple-element.15), channel_id=1, source_target_pairs={{0,4},{1,5},{2,6},{3,7},{8,12},{9,13},{10,14},{11,15},{16,20},{17,... | collective-permute-start | bytes 491528 | tf_op jit(solution)/shard_map/ppermute | solution.py:14
  134.1 3.3 %collective-permute-start.2 = (f32[32,10,1,128]{3,0,2,1:T(8,128)S(1)}, f32[32,10,1,128]{3,0,2,1:T(8,128)S(1)}, u32[]{:S(2)}, u32[]{:S(2)}) collective-permute-start(f32[32,10,1,128]{3,0,2,1:T(8,128)S(1)} %get-tuple-element.16), channel_id=1, source_target_pairs={{4,0},{5,1},{6,2},{7,3},{12,8},{13,9},{14,10},{15,11},{20,16},{21,... | collective-permute-start | bytes 491528 | tf_op jit(solution)/shard_map/ppermute | solution.py:17
  135.4 2.2 copy-start.3
  137.4 0.7 copy-start.5
  142.4 7.9 %collective-permute-start.4 = (f32[32,10,10,1]{0,3,2,1:T(1,128)S(1)}, f32[32,10,10,1]{0,3,2,1:T(1,128)S(1)}, u32[]{:S(2)}, u32[]{:S(2)}) collective-permute-start(f32[32,10,10,1]{0,3,2,1:T(1,128)S(1)} %copy.13), channel_id=1, source_target_pairs={{1,0},{2,1},{3,2},{5,4},{6,5},{7,6},{9,8},{10,9},{11,10},{13,12},{... | collective-permute-start | bytes 38408 | tf_op jit(solution)/shard_map/ppermute | solution.py:17
  145.8 6.4 %collective-permute-start.5 = (f32[32,10,10,1]{0,3,2,1:T(1,128)S(1)}, f32[32,10,10,1]{0,3,2,1:T(1,128)S(1)}, u32[]{:S(2)}, u32[]{:S(2)}) collective-permute-start(f32[32,10,10,1]{0,3,2,1:T(1,128)S(1)} %copy.15), channel_id=1, source_target_pairs={{0,1},{1,2},{2,3},{4,5},{5,6},{6,7},{8,9},{9,10},{10,11},{12,13},{... | collective-permute-start | bytes 38408 | tf_op jit(solution)/shard_map/ppermute | solution.py:14
  157.0 6.4 %collective-permute-start.7 = (f32[32,1,8,128]{3,0,2,1:T(8,128)S(1)}, f32[32,1,8,128]{3,0,2,1:T(8,128)S(1)}, u32[]{:S(2)}, u32[]{:S(2)}) collective-permute-start(f32[32,1,8,128]{3,0,2,1:T(8,128)S(1)} %get-tuple-element.19), channel_id=1, source_target_pairs={{0,8},{8,16},{16,24},{1,9},{9,17},{17,25},{2,10},{10,18},{18,26},{... | collective-permute-start | bytes 393224 | tf_op jit(solution)/shard_map/ppermute | solution.py:14
  160.9 6.9 %collective-permute-start.6 = (f32[32,1,8,128]{3,0,2,1:T(8,128)S(1)}, f32[32,1,8,128]{3,0,2,1:T(8,128)S(1)}, u32[]{:S(2)}, u32[]{:S(2)}) collective-permute-start(f32[32,1,8,128]{3,0,2,1:T(8,128)S(1)} %get-tuple-element.20), channel_id=1, source_target_pairs={{8,0},{16,8},{24,16},{9,1},{17,9},{25,17},{10,2},{18,10},{26,18},{... | collective-permute-start | bytes 393224 | tf_op jit(solution)/shard_map/ppermute | solution.py:17
  167.8 2.6 %collective-permute-start.9 = (f32[32,10,1,128]{3,0,2,1:T(8,128)S(1)}, f32[32,10,1,128]{3,0,2,1:T(8,128)S(1)}, u32[]{:S(2)}, u32[]{:S(2)}) collective-permute-start(f32[32,10,1,128]{3,0,2,1:T(8,128)S(1)} %get-tuple-element.13), channel_id=1, source_target_pairs={{0,4},{1,5},{2,6},{3,7},{8,12},{9,13},{10,14},{11,15},{16,20},{17,... | collective-permute-start | bytes 491528 | tf_op jit(solution)/shard_map/ppermute | solution.py:14
  169.1 3.3 %collective-permute-start.8 = (f32[32,10,1,128]{3,0,2,1:T(8,128)S(1)}, f32[32,10,1,128]{3,0,2,1:T(8,128)S(1)}, u32[]{:S(2)}, u32[]{:S(2)}) collective-permute-start(f32[32,10,1,128]{3,0,2,1:T(8,128)S(1)} %get-tuple-element.14), channel_id=1, source_target_pairs={{4,0},{5,1},{6,2},{7,3},{12,8},{13,9},{14,10},{15,11},{20,16},{21,... | collective-permute-start | bytes 491528 | tf_op jit(solution)/shard_map/ppermute | solution.py:17
  170.5 2.0 copy-start.4
  172.4 0.7 copy-start.6
  177.6 8.2 %collective-permute-start.10 = (f32[32,10,10,1]{0,3,2,1:T(1,128)S(1)}, f32[32,10,10,1]{0,3,2,1:T(1,128)S(1)}, u32[]{:S(2)}, u32[]{:S(2)}) collective-permute-start(f32[32,10,10,1]{0,3,2,1:T(1,128)S(1)} %copy.17), channel_id=1, source_target_pairs={{1,0},{2,1},{3,2},{5,4},{6,5},{7,6},{9,8},{10,9},{11,10},{13,12},{... | collective-permute-start | bytes 38408 | tf_op jit(solution)/shard_map/ppermute | solution.py:17
  181.0 6.6 %collective-permute-start.11 = (f32[32,10,10,1]{0,3,2,1:T(1,128)S(1)}, f32[32,10,10,1]{0,3,2,1:T(1,128)S(1)}, u32[]{:S(2)}, u32[]{:S(2)}) collective-permute-start(f32[32,10,10,1]{0,3,2,1:T(1,128)S(1)} %copy.19), channel_id=1, source_target_pairs={{0,1},{1,2},{2,3},{4,5},{5,6},{6,7},{8,9},{9,10},{10,11},{12,13},{... | collective-permute-start | bytes 38408 | tf_op jit(solution)/shard_map/ppermute | solution.py:14
  192.4 5.6 %collective-permute-start.13 = (f32[32,1,8,128]{3,0,2,1:T(8,128)S(1)}, f32[32,1,8,128]{3,0,2,1:T(8,128)S(1)}, u32[]{:S(2)}, u32[]{:S(2)}) collective-permute-start(f32[32,1,8,128]{3,0,2,1:T(8,128)S(1)} %get-tuple-element.17), channel_id=1, source_target_pairs={{0,8},{8,16},{16,24},{1,9},{9,17},{17,25},{2,10},{10,18},{18,26},{... | collective-permute-start | bytes 393224 | tf_op jit(solution)/shard_map/ppermute | solution.py:14
  195.2 6.9 %collective-permute-start.12 = (f32[32,1,8,128]{3,0,2,1:T(8,128)S(1)}, f32[32,1,8,128]{3,0,2,1:T(8,128)S(1)}, u32[]{:S(2)}, u32[]{:S(2)}) collective-permute-start(f32[32,1,8,128]{3,0,2,1:T(8,128)S(1)} %get-tuple-element.18), channel_id=1, source_target_pairs={{8,0},{16,8},{24,16},{9,1},{17,9},{25,17},{10,2},{18,10},{26,18},{... | collective-permute-start | bytes 393224 | tf_op jit(solution)/shard_map/ppermute | solution.py:17
  202.2 2.6 %collective-permute-start.15 = (f32[32,10,1,128]{3,0,2,1:T(8,128)S(1)}, f32[32,10,1,128]{3,0,2,1:T(8,128)S(1)}, u32[]{:S(2)}, u32[]{:S(2)}) collective-permute-start(f32[32,10,1,128]{3,0,2,1:T(8,128)S(1)} %get-tuple-element.11), channel_id=1, source_target_pairs={{0,4},{1,5},{2,6},{3,7},{8,12},{9,13},{10,14},{11,15},{16,20},{17,... | collective-permute-start | bytes 491528 | tf_op jit(solution)/shard_map/ppermute | solution.py:14
  203.5 3.3 %collective-permute-start.14 = (f32[32,10,1,128]{3,0,2,1:T(8,128)S(1)}, f32[32,10,1,128]{3,0,2,1:T(8,128)S(1)}, u32[]{:S(2)}, u32[]{:S(2)}) collective-permute-start(f32[32,10,1,128]{3,0,2,1:T(8,128)S(1)} %get-tuple-element.12), channel_id=1, source_target_pairs={{4,0},{5,1},{6,2},{7,3},{12,8},{13,9},{14,10},{15,11},{20,16},{21,... | collective-permute-start | bytes 491528 | tf_op jit(solution)/shard_map/ppermute | solution.py:17
  204.8 2.2 copy-start.7
  206.8 0.7 copy-start.8
  211.7 9.5 %collective-permute-start.16 = (f32[32,10,10,1]{0,3,2,1:T(1,128)S(1)}, f32[32,10,10,1]{0,3,2,1:T(1,128)S(1)}, u32[]{:S(2)}, u32[]{:S(2)}) collective-permute-start(f32[32,10,10,1]{0,3,2,1:T(1,128)S(1)} %copy.21), channel_id=1, source_target_pairs={{1,0},{2,1},{3,2},{5,4},{6,5},{7,6},{9,8},{10,9},{11,10},{13,12},{... | collective-permute-start | bytes 38408 | tf_op jit(solution)/shard_map/ppermute | solution.py:17
  215.7 10.0 %copy-start.2 = (f32[32,8,8,128]{3,2,1,0:T(8,128)S(1)}, f32[32,8,8,128]{3,2,1,0:T(8,128)}, u32[]{:S(2)}) copy-start(f32[32,8,8,128]{3,2,1,0:T(8,128)} %param.8) | copy-start | bytes 3145732
  215.7 7.4 %collective-permute-start.17 = (f32[32,10,10,1]{0,3,2,1:T(1,128)}, f32[32,10,10,1]{0,3,2,1:T(1,128)}, u32[]{:S(2)}, u32[]{:S(2)}) collective-permute-start(f32[32,10,10,1]{0,3,2,1:T(1,128)} %copy.23), channel_id=1, source_target_pairs={{0,1},{1,2},{2,3},{4,5},{5,6},{6,7},{8,9},{9,10},{10,11},{12,13},{... | collective-permute-start | bytes 38408 | tf_op jit(solution)/shard_map/ppermute | solution.py:14
Sparse Core Ops, SparseCore 0:
  14.3 57.6 all-reduce.2
  74.9 41.2 all-reduce.4
